TPU v7x, 32 devices: a whole 2x2x4 slice. The times are simulated.
32 devices in a mesh: dp: 8 (over y, x, core), tensor: 4 (over z).
Axes of the slice: x: 2, y: 2, z: 4, core: 2. Of those that a mesh axis runs over, the one named last changes fastest.
Arguments:
- tokens: bfloat16 [128, 8192], P('dp'), may hold values from -6 to 6
- norm_gain: bfloat16 [8192], replicated, may hold values from 0.099609375 to 1.8984375
- w_query: bfloat16 [8192, 8192], P('dp', 'tensor'), may hold values from -0.0625 to 0.0625
- w_key: bfloat16 [8192, 1024], P('dp', 'tensor'), may hold values from -0.0625 to 0.0625
- w_value: bfloat16 [8192, 1024], P('dp', 'tensor'), may hold values from -0.0625 to 0.0625
- check_column: bfloat16 [8192], replicated, may hold values from -6 to 6
- key_cache: bfloat16 [4096, 16, 8, 128], P('dp', None, 'tensor'), may hold values from -320 to 320
- value_cache: bfloat16 [4096, 16, 8, 128], P('dp', None, 'tensor'), may hold values from -6 to 6
- page_table: int32 [128, 32], P('dp'), may hold values from 0 to 511, as said below
- lengths: int32 [128], P('dp'), may hold values from 1 to 512, as said below
- tol_counts: int32 [128], replicated, may hold values from 0 to 7
Outputs:
- attention: bfloat16 [128, 8192], P('dp', 'tensor')
- excess: float32 [], replicated
Inputs may be any that keep to these rules, and one draw needn't show every extreme that they name: page_table holds pool pages of the index of dp that holds the sequence; the 16 sequences of one index of dp own distinct pages and together own all 512 of them. `lengths`: some sequence holds exactly 512 cached tokens.
All inputs are finite; a program needn't handle non-finite values.
Results may differ from a plain program's by a relative error of at most 0.007.
The roundings to bfloat16 on the way count: a program that leaves them out, or rounds other values in their place, can miss the bound.
Values may be sent and summed in bfloat16 or wider, within the bound.
A program may use at most 64 MiB of HBM per device.

v0:
```python
import math

import jax
import jax.numpy as jnp
from jax import lax
from jax.sharding import PartitionSpec as P

HQ = 64
KVH = 8
HD = 128


epsilon = 1e-06
rope_base = 1000000.0
tol_step = 0.25


def normalize(tokens, norm_gain):
    widened = tokens.astype(jnp.float32)
    mean_square = jnp.mean(widened * widened, axis=1, keepdims=True)
    return (widened * lax.rsqrt(mean_square + epsilon) * norm_gain.astype(jnp.float32)).astype(
        jnp.bfloat16
    )


def rotate(vectors, positions):
    half_width = vectors.shape[-1] // 2
    steps_index = jnp.arange(half_width, dtype=jnp.float32)
    inverse = rope_base ** (-2.0 * steps_index / vectors.shape[-1])
    angles = positions.astype(jnp.float32)[:, None] * inverse[None, :]
    cosine = jnp.cos(angles)[:, None, :]
    sine_part = jnp.sin(angles)[:, None, :]
    lower = vectors[..., :half_width]
    upper = vectors[..., half_width:]
    return jnp.concatenate(
        [lower * cosine - upper * sine_part, upper * cosine + lower * sine_part], axis=-1
    )


def attend(query_heads, cached_keys, cached_values, key_new, value_new, lengths):
    score_scale = query_heads.shape[-1] ** (-0.5)
    scores = (
        jnp.einsum("skgd,sckd->skgc", query_heads, cached_keys, preferred_element_type=jnp.float32)
        * score_scale
    )
    new_score = (
        jnp.einsum("skgd,skd->skg", query_heads, key_new, preferred_element_type=jnp.float32)
        * score_scale
    )
    live_mask = (jnp.arange(cached_keys.shape[1])[None, :] < lengths[:, None])[:, None, None, :]
    masked = jnp.where(live_mask, scores, -jnp.inf)
    peak_score = jnp.maximum(jnp.max(masked, axis=-1), new_score)
    weights = jnp.exp(masked - peak_score[..., None])
    new_weight = jnp.exp(new_score - peak_score)
    denominator = jnp.sum(weights, axis=-1) + new_weight
    rounded_new = lax.optimization_barrier(new_weight.astype(jnp.bfloat16)).astype(jnp.float32)
    mixed_heads = jnp.einsum(
        "skgc,sckd->skgd",
        weights.astype(jnp.bfloat16),
        cached_values,
        preferred_element_type=jnp.float32,
    )
    mixed_heads = (
        mixed_heads + rounded_new[..., None] * value_new.astype(jnp.float32)[:, :, None, :]
    )
    return mixed_heads / denominator[..., None]


def body(
    tokens,
    norm_gain,
    w_query,
    w_key,
    w_value,
    check_column,
    key_cache,
    value_cache,
    page_table,
    lengths,
    tol_counts,
):
    seq_rows = tokens.shape[0]
    head_size = key_cache.shape[-1]
    normed = normalize(tokens, norm_gain)
    spread = lax.all_to_all(normed, "dp", split_axis=1, concat_axis=0, tiled=True)
    projected = lax.psum_scatter(
        jnp.concatenate(
            [
                jnp.dot(spread, w_query, preferred_element_type=jnp.float32),
                jnp.dot(spread, w_key, preferred_element_type=jnp.float32),
                jnp.dot(spread, w_value, preferred_element_type=jnp.float32),
            ],
            axis=1,
        ),
        "dp",
        scatter_dimension=0,
        tiled=True,
    )
    column_count = (HQ + 2 * KVH) * HD
    local_sums = jnp.sum(projected, axis=1)
    check_sums = jnp.dot(normed, check_column, preferred_element_type=jnp.float32)
    all_rows = seq_rows * lax.axis_size("dp")
    block_total = lax.psum(local_sums, "tensor")
    residual = (block_total - check_sums) / math.sqrt(column_count)
    own_counts = lax.dynamic_slice_in_dim(tol_counts, lax.axis_index("dp") * seq_rows, seq_rows, 0)
    token_excess = jnp.maximum(jnp.abs(residual) - tol_step * own_counts.astype(jnp.float32), 0.0)
    excess = lax.psum(jnp.sum(token_excess), "dp") / math.sqrt(all_rows)
    query_width = w_query.shape[1]
    kv_width = w_key.shape[1]
    heads_here = query_width // head_size
    kv_here = kv_width // head_size
    group_size = heads_here // kv_here
    query_heads = rotate(
        projected[:, :query_width].reshape(seq_rows, heads_here, head_size), lengths
    ).astype(jnp.bfloat16)
    key_new = rotate(
        projected[:, query_width : query_width + kv_width].reshape(seq_rows, kv_here, head_size),
        lengths,
    ).astype(jnp.bfloat16)
    value_new = (
        projected[:, query_width + kv_width :]
        .reshape(seq_rows, kv_here, head_size)
        .astype(jnp.bfloat16)
    )
    context = page_table.shape[1] * key_cache.shape[1]
    cached_keys = key_cache[page_table].reshape(seq_rows, context, kv_here, head_size)
    cached_values = value_cache[page_table].reshape(seq_rows, context, kv_here, head_size)
    mixed_heads = attend(
        query_heads.reshape(seq_rows, kv_here, group_size, head_size),
        cached_keys,
        cached_values,
        key_new,
        value_new,
        lengths,
    )
    attention = mixed_heads.reshape(seq_rows, heads_here * head_size).astype(jnp.bfloat16)
    return (attention, excess)


def solution(mesh):
    return jax.shard_map(
        body,
        mesh=mesh,
        in_specs=(
            P("dp", None),
            P(),
            P("dp", "tensor"),
            P("dp", "tensor"),
            P("dp", "tensor"),
            P(),
            P("dp", None, "tensor", None),
            P("dp", None, "tensor", None),
            P("dp", None),
            P("dp"),
            P(),
        ),
        out_specs=(P("dp", "tensor"), P()),
        check_vma=False,
    )
```

profile of v0, /device:TPU:0, one launch (start us, length us, event | category | flops | bytes accessed | tf_op | source)
XLA Modules:
  0.0 112.8 jit_solution(3940813790565365840)
XLA Ops:
  7.2 0.0 copy-start
  7.2 0.0 reduce-scatter.2.cloned.1.call-start
  7.2 0.8 convert_element_type.51
  8.0 1.1 fusion.25
  9.2 1.1 fusion.27
  10.3 11.9 %all_to_all.19 = bf16[16,8,1024]{2,0,1:T(8,128)(2,1)S(1)} all-to-all(bf16[16,8,1024]{2,0,1:T(8,128)(2,1)S(1)} %bitcast.54), channel_id=1, replica_groups=mesh['dp'=8,'tensor'=4] {'dp'}, dimensions={1} | all-to-all | bytes 524288 | tf_op jit(solution)/shard_map/all_to_all | solution.py:85
  22.2 2.9 %fusion.42 = f32[128,2048]{1,0:T(8,128)S(1)} fusion(bf16[128,1024]{1,0:T(8,128)(2,1)S(1)} %bitcast.49, bf16[1024,2048]{1,0:T(8,128)(2,1)} %param.13), kind=kOutput, calls=%fused_computation.57 | convolution fusion | flops 536870912 | bytes 5505024 | tf_op jit(solution)/shard_map/dot_general | solution.py:89
  25.1 0.2 fusion.43
  25.4 0.2 fusion.44
  25.7 1.3 %pad_maximum_fusion = f32[128,2560]{1,0:T(8,128)} fusion(f32[128,256]{1,0:T(8,128)S(1)} %fusion.44, f32[128,256]{1,0:T(8,128)S(1)} %fusion.43, f32[128,2048]{1,0:T(8,128)S(1)} %fusion.42), kind=kLoop, calls=%fused_computation.6 | loop fusion | flops 655360 | bytes 2621440 | tf_op jit(solution)/shard_map/concatenate | solution.py:87
  26.9 0.0 reduce-scatter.2.cloned.1.call-update
  27.0 0.1 reshape.122
  27.1 20.9 %gather_fusion = bf16[512,16,2,128]{3,2,1,0:T(2,128)(2,1)} fusion(bf16[512,16,2,128]{3,2,1,0:T(2,128)(2,1)} %param.17, s32[1024]{0:T(1024)S(1)} %pad_clamp_fusion), kind=kCustom, calls=%fused_computation | custom fusion | bytes 8390656 | tf_op jit(solution)/shard_map/gather | solution.py:126
  47.9 20.9 %gather_fusion.1 = bf16[512,16,2,128]{3,2,1,0:T(2,128)(2,1)} fusion(bf16[512,16,2,128]{3,2,1,0:T(2,128)(2,1)} %param.18, s32[1024]{0:T(1024)S(1)} %pad_clamp_fusion), kind=kCustom, calls=%fused_computation.1 | custom fusion | bytes 8390656 | tf_op jit(solution)/shard_map/gather | solution.py:127
  68.9 0.1 iota_compare_fusion
  68.9 0.1 multiply_cosine_fusion
  69.1 0.0 reduce-scatter.2.cloned.1.call-done
  69.1 0.8 slice.36
  69.9 0.9 slice_bitcast_fusion
  70.9 0.1 subtract_convert_fusion.1
  71.0 0.1 fusion.32
  71.1 0.1 maximum_bitcast_fusion
  71.2 0.2 fusion.34
  71.4 3.5 %fusion.41 = (f32[16,2,8]{2,1,0:T(2,128)S(1)}, f32[16,2,8,512]{3,2,1,0:T(8,128)S(1)}) fusion(bf16[16,512,2,128]{3,2,1,0:T(2,128)(2,1)} %bitcast.47, bf16[16,2,8,64]{3,2,1,0:T(8,128)(2,1)S(1)} %get-tuple-element.3, bf16[16,2,8,64]{3,2,1,0:T(8,128)(2,1)S(1)} %get-tuple-element.2, pred[16,512]{1,0:T(8,128)(4,1)S(1)} %iota_compare_fusion), kind=kOutput, calls=%fused_computation.56 | convolution fusion | flops 34078464 | bytes 4793344 | tf_op jit(solution)/shard_map/skgd,sckd->skgc/dot_general | solution.py:43
  74.9 0.0 copy-start.6
  74.9 0.2 fusion.28
  75.3 0.1 reduce_sum.38
  75.4 12.0 %psum.14 = f32[16]{0:T(128)S(1)} all-reduce(f32[16]{0:T(128)S(1)} %reduce_sum.38), channel_id=1, replica_groups=mesh['dp'=8,'tensor'=4] {'tensor'}, use_global_device_ids=true, to_apply=%region_5.0 | all-reduce | flops 16 | bytes 128 | tf_op jit(solution)/shard_map/psum | solution.py:103
  87.4 2.9 %fusion.16 = bf16[16,2,8,128]{3,2,1,0:T(8,128)(2,1)S(1)} fusion(bf16[16,512,2,128]{3,2,1,0:T(2,128)(2,1)} %bitcast.48, f32[16,2,8,512]{3,2,1,0:T(8,128)S(1)} %get-tuple-element.11, f32[16,2,8]{2,1,0:T(2,128)S(1)} %multiply_maximum_fusion, f32[16,2,8]{2,1,0:T(2,128)S(1)} %get-tuple-element.5, f32[16,2,128]{2,1,0:T(2,128)S(1)} %reshape.119, ...), kind=kOutput, calls=%fused_computation.11 | convolution fusion | flops 33947648 | bytes 4803584 | tf_op jit(solution)/shard_map/skgc,sckd->skgd/dot_general | solution.py:57
  90.3 0.8 fusion.24
  91.1 0.6 copy.49
  91.7 12.4 %psum.15 = f32[]{:T(128)} all-reduce(f32[]{:T(128)} %fusion.24), channel_id=1, replica_groups=mesh['dp'=8,'tensor'=4] {'dp'}, use_global_device_ids=true, to_apply=%region_7.8 | all-reduce | flops 1 | bytes 8 | tf_op jit(solution)/shard_map/psum | solution.py:107
  (26 shorter events, 0.2 us)
Async XLA Ops:
  7.2 18.0 %copy-start = (bf16[1024,256]{1,0:T(8,128)(2,1)S(1)}, bf16[1024,256]{1,0:T(8,128)(2,1)}, u32[]{:S(2)}) copy-start(bf16[1024,256]{1,0:T(8,128)(2,1)} %param.14) | copy-start | bytes 1572868
  7.2 18.2 %copy-start.2 = (bf16[1024,256]{1,0:T(8,128)(2,1)S(1)}, bf16[1024,256]{1,0:T(8,128)(2,1)}, u32[]{:S(2)}) copy-start(bf16[1024,256]{1,0:T(8,128)(2,1)} %param.15) | copy-start | bytes 1572868
  7.2 61.9 %reduce-scatter.2.cloned.1.call-start = ((), (), s32[]{:S(2)}) async-start(), calls=%async_computation.2 | async-start | bytes 1474560 | tf_op jit(solution)/shard_map/reduce_scatter | solution.py:86
  25.1 1.8 %copy-start.5 = (s32[16]{0:T(128)S(1)}, s32[16]{0:T(128)}, u32[]{:S(2)}) copy-start(s32[16]{0:T(128)} %param.20) | copy-start | bytes 196
  25.1 1.8 %copy-start.4 = (s32[16,32]{1,0:T(8,128)S(1)}, s32[16,32]{1,0:T(8,128)}, u32[]{:S(2)}) copy-start(s32[16,32]{1,0:T(8,128)} %param.19) | copy-start | bytes 6148
  47.9 20.9 %copy-start.3 = (bf16[8192]{0:T(1024)(128)(2,1)S(1)}, bf16[8192]{0:T(1024)(128)(2,1)}, u32[]{:S(2)}) copy-start(bf16[8192]{0:T(1024)(128)(2,1)} %param.16) | copy-start | bytes 49156
  69.1 6.1 %copy-start.1 = (f32[16,2560]{1,0:T(8,128)S(1)}, f32[16,2560]{1,0:T(8,128)}, u32[]{:S(2)}) copy-start(f32[16,2560]{1,0:T(8,128)} %reduce-scatter.2.cloned.1.call-done) | copy-start | bytes 491524
  74.9 15.4 %copy-start.6 = (s32[128]{0:T(128)S(1)}, s32[128]{0:T(128)}, u32[]{:S(2)}) copy-start(s32[128]{0:T(128)} %param.21) | copy-start | bytes 1540
Sparse Core Ops, SparseCore 0:
  27.1 36.5 reduce-scatter.1
where the time goes:
time: 113 us
  local copies, waits for them, and re-layouts  44.3 us (39%)
  blocking collectives  36.3 us (32%)
  between operations  16.1 us (14%)
  matrix products  10.8 us (10%)
  other arithmetic  5.21 us (5%)
    gather x1, local copies, waits for them, and re-layouts, body(): value_cache[page_table].reshape(seq_rows, context, kv_here, head_size)  20.9 us
    gather x1, local copies, waits for them, and re-layouts, body(): key_cache[page_table].reshape(seq_rows, context, kv_here, head_size)  20.9 us
    psum x1, blocking collectives, body(): excess = lax.psum(jnp.sum(token_excess), 'dp') / math.sqrt(all_rows)  12.4 us
    psum x1, blocking collectives, body(): block_total = lax.psum(local_sums, 'tensor')  12 us
    all_to_all x1, blocking collectives, body(): lax.all_to_all(normed, 'dp', split_axis=1, concat_axis=0, tiled=True)  11.9 us
    dot_general x1, matrix products, attend(): jnp.einsum('skgd,sckd->skgc', query_heads, cached_keys, preferred_element...  3.52 us
    dot_general x1, matrix products, body(): jnp.dot(spread, w_query, preferred_element_type=jnp.float32)  2.92 us
    dot_general x1, matrix products, attend(): jnp.einsum('skgc,sckd->skgd', weights.astype(jnp.bfloat16), cached_values...  2.89 us
  transfers between devices with their start and end apart: 1, of which 0 were waited for; matrix products, arithmetic and copies ran while one was open for 37% of the time, Pallas kernels for 0%

commit v1 on v0

v1 whole, which is shorter than its diff:
```python
import functools
import math

import jax
import jax.numpy as jnp
from jax import lax
from jax.experimental import pallas as pl
from jax.experimental.pallas import tpu as pltpu
from jax.sharding import PartitionSpec as P

EPSILON = 1e-06
ROPE_BASE = 1000000.0
TOL_STEP = 0.25
MESH = pl.DeviceIdType.MESH
F32 = jnp.float32
BF16 = jnp.bfloat16
UNROLL = 4


def step_kernel(
    dp,
    tp,
    table_ref,
    lengths_ref,
    counts_ref,
    tokens_ref,
    gain_ref,
    check_ref,
    cos_ref,
    sin_ref,
    wq_hbm,
    wk_hbm,
    wv_hbm,
    keys_hbm,
    values_hbm,
    out_ref,
    excess_ref,
    weights,
    keys,
    values,
    outgoing,
    spread,
    parts,
    from_pair,
    from_chips,
    queries,
    new_keys,
    new_values,
    mixed,
    sums_all,
    sums_own,
    excess_all,
    excess_own,
    load_sems,
    a2a_send,
    a2a_recv,
    pair_send,
    pair_recv,
    chip_send,
    chip_recv,
    sum_send,
    sum_recv,
    exc_send,
    exc_recv,
):
    chips = dp // 2
    me = lax.axis_index("dp")
    zed = lax.axis_index("tensor")
    chip, core = me // 2, me % 2
    seqs, width = tokens_ref.shape
    depth = width // dp
    q_width, kv_width = wq_hbm.shape[1], wk_hbm.shape[1]
    total = q_width + 2 * kv_width
    chunks, _, _, chunk = parts.shape
    head = keys_hbm.shape[2]
    q_heads, kv_heads = q_width // head, kv_width // head
    group = q_heads // kv_heads
    pages = table_ref.shape[1]
    page_rows = keys_hbm.shape[1]

    barrier = pltpu.get_barrier_semaphore()
    for k in range(1, dp):
        pl.semaphore_signal(
            barrier, inc=1, device_id=((me + k) % dp, zed), device_id_type=MESH
        )
    for k in range(1, tp):
        pl.semaphore_signal(
            barrier, inc=1, device_id=(me, (zed + k) % tp), device_id_type=MESH
        )

    loads = [
        pltpu.make_async_copy(wq_hbm, weights.at[:, pl.ds(0, q_width)], load_sems.at[0]),
        pltpu.make_async_copy(wk_hbm, weights.at[:, pl.ds(q_width, kv_width)], load_sems.at[1]),
        pltpu.make_async_copy(
            wv_hbm, weights.at[:, pl.ds(q_width + kv_width, kv_width)], load_sems.at[2]
        ),
        pltpu.make_async_copy(keys_hbm, keys, load_sems.at[3]),
        pltpu.make_async_copy(values_hbm, values, load_sems.at[4]),
    ]
    for load in loads:
        load.start()

    square = jnp.zeros((seqs, 1), F32)
    for j in range(dp):
        cols = pl.ds(j * depth, depth)
        part = tokens_ref[:, cols].astype(F32)
        square = square + jnp.sum(part * part, axis=1, keepdims=True)
    scale = lax.rsqrt(square / width + EPSILON)
    for j in range(dp):
        cols = pl.ds(j * depth, depth)
        outgoing[j] = (
            tokens_ref[:, cols].astype(F32) * scale * gain_ref[:, cols].astype(F32)
        ).astype(BF16)
    spread[0, 0] = outgoing[me]

    pl.semaphore_wait(barrier, dp - 1 + tp - 1)

    a2a = []
    for dc in range(chips - 1, -1, -1):
        for q in range(2):
            if dc == 0 and q == 0:
                continue
            target = ((chip + dc) % chips) * 2 + (core + q) % 2
            copy = pltpu.make_async_remote_copy(
                src_ref=outgoing.at[target],
                dst_ref=spread.at[q, dc],
                send_sem=a2a_send.at[q, dc],
                recv_sem=a2a_recv.at[q, dc],
                device_id=(target, zed),
                device_id_type=MESH,
            )
            copy.start()
            a2a.append(copy)

    check_sum = jnp.zeros((seqs, 1), F32)
    for j in range(dp):
        cols = pl.ds(j * depth, depth)
        check_sum = check_sum + jnp.sum(
            outgoing[j].astype(F32) * check_ref[:, cols].astype(F32), axis=1, keepdims=True
        )

    for load in loads[:3]:
        load.wait()
    for copy in a2a:
        copy.wait_recv()

    pair_copies, chip_copies = [], []
    half = chips * seqs

    def project(c):
        product = jnp.dot(
            spread[...].reshape(dp * seqs, depth),
            weights[:, pl.ds(c * chunk, chunk)],
            preferred_element_type=F32,
        )
        parts[c, 1] = product[half:]
        copy = pltpu.make_async_remote_copy(
            src_ref=parts.at[c, 1],
            dst_ref=from_pair.at[c],
            send_sem=pair_send.at[c],
            recv_sem=pair_recv.at[c],
            device_id=(chip * 2 + (core + 1) % 2, zed),
            device_id_type=MESH,
        )
        copy.start()
        pair_copies.append(copy)
        parts[c, 0] = product[:half]

    def pass_on(c):
        pair_copies[c].wait_recv()
        for dc in range(chips - 1, 0, -1):
            rows = pl.ds(dc * seqs, seqs)
            parts[c, 0, rows] = parts[c, 0, rows] + from_pair[c, rows]
            copy = pltpu.make_async_remote_copy(
                src_ref=parts.at[c, 0, rows],
                dst_ref=from_chips.at[c, dc - 1],
                send_sem=chip_send.at[c, dc - 1],
                recv_sem=chip_recv.at[c, dc - 1],
                device_id=(((chip + chips - dc) % chips) * 2 + core, zed),
                device_id_type=MESH,
            )
            copy.start()
            chip_copies.append(copy)

    for c in range(chunks):
        project(c)
        if c >= 1:
            pass_on(c - 1)
    pass_on(chunks - 1)

    def rotate(vector):
        return (
            (vector * cos_ref[...] + pltpu.roll(vector, head // 2, 1) * sin_ref[...])
            .astype(BF16)
            .astype(F32)
        )

    local_sum = jnp.zeros((seqs, 1), F32)
    for c in range(chunks):
        for copy in chip_copies[c * (chips - 1) : (c + 1) * (chips - 1)]:
            copy.wait_recv()
        own = parts[c, 0, pl.ds(0, seqs)] + from_pair[c, pl.ds(0, seqs)]
        for dc in range(1, chips):
            own = own + from_chips[c, dc - 1]
        local_sum = local_sum + jnp.sum(own, axis=1, keepdims=True)
        for i in range(chunk // head):
            block = own[:, i * head : (i + 1) * head]
            index = c * (chunk // head) + i
            if index < q_heads:
                queries[:, index, :] = rotate(block)
            elif index < q_heads + kv_heads:
                k = index - q_heads
                turned = rotate(block)
                for g in range(group):
                    new_keys[:, k * group + g, :] = turned
            else:
                k = index - q_heads - kv_heads
                rounded = block.astype(BF16).astype(F32)
                for g in range(group):
                    new_values[:, k * group + g, :] = rounded

    sums_own[...] = jnp.broadcast_to(local_sum, sums_own.shape)
    sums_all[zed] = sums_own[...]
    sum_copies = []
    for k in range(1, tp):
        copy = pltpu.make_async_remote_copy(
            src_ref=sums_own,
            dst_ref=sums_all.at[zed],
            send_sem=sum_send.at[k],
            recv_sem=sum_recv.at[k],
            device_id=(me, (zed + k) % tp),
            device_id_type=MESH,
        )
        copy.start()
        sum_copies.append(copy)

    span = pages * page_rows
    column = lax.broadcasted_iota(jnp.int32, (q_heads, span), 1)
    row = lax.broadcasted_iota(jnp.int32, (q_heads, span), 0)
    place = jnp.where(column % kv_heads == row // group, column // kv_heads, span)
    score_scale = head ** (-0.5)
    for load in loads[3:]:
        load.wait()

    def one_sequence(s, carry):
        owned = [table_ref[s, p] for p in range(pages)]
        length = lengths_ref[s]
        query = queries[s]
        cached = jnp.concatenate([keys[page] for page in owned], axis=0)
        scores = (
            lax.dot_general(
                query.astype(BF16),
                cached,
                (((1,), (1,)), ((), ())),
                preferred_element_type=F32,
            )
            * score_scale
        )
        new_score = jnp.sum(query * new_keys[s], axis=1, keepdims=True) * score_scale
        masked = jnp.where(place < length, scores, -jnp.inf)
        peak = jnp.maximum(jnp.max(masked, axis=1, keepdims=True), new_score)
        soft = jnp.exp(masked - peak)
        new_weight = jnp.exp(new_score - peak)
        denominator = jnp.sum(soft, axis=1, keepdims=True) + new_weight
        stored = jnp.concatenate([values[page] for page in owned], axis=0)
        result = jnp.dot(soft.astype(BF16), stored, preferred_element_type=F32)
        result = result + new_weight.astype(BF16).astype(F32) * new_values[s]
        mixed[s] = result / denominator
        return carry

    middle = seqs // 2
    lax.fori_loop(0, middle, one_sequence, 0, unroll=UNROLL)

    for copy in sum_copies:
        copy.wait_recv()
    row_sums = sums_all[0]
    for k in range(1, tp):
        row_sums = row_sums + sums_all[k]
    seq_row = lax.broadcasted_iota(jnp.int32, (seqs, sums_own.shape[1]), 0)
    counts = jnp.zeros(seq_row.shape, F32)
    for s in range(seqs):
        counts = jnp.where(seq_row == s, counts_ref[me * seqs + s].astype(F32), counts)
    residual = (row_sums - check_sum) / math.sqrt(total * tp)
    over = jnp.maximum(jnp.abs(residual) - TOL_STEP * counts, 0.0)
    excess_own[...] = jnp.broadcast_to(jnp.sum(over, axis=0, keepdims=True), excess_own.shape)
    excess_all[me] = excess_own[...]
    exc_copies = []
    for k in range(1, dp):
        copy = pltpu.make_async_remote_copy(
            src_ref=excess_own,
            dst_ref=excess_all.at[me],
            send_sem=exc_send.at[k],
            recv_sem=exc_recv.at[k],
            device_id=((me + k) % dp, zed),
            device_id_type=MESH,
        )
        copy.start()
        exc_copies.append(copy)

    lax.fori_loop(middle, seqs, one_sequence, 0, unroll=UNROLL)

    for h in range(q_heads):
        out_ref[:, h * head : (h + 1) * head] = mixed[:, h, :].astype(BF16)

    for copy in exc_copies:
        copy.wait_recv()
    grand = excess_all[0]
    for k in range(1, dp):
        grand = grand + excess_all[k]
    excess_ref[...] = grand / math.sqrt(seqs * dp)

    for copy in a2a + pair_copies + chip_copies + sum_copies + exc_copies:
        copy.wait_send()


def body(
    dp,
    tp,
    tokens,
    norm_gain,
    w_query,
    w_key,
    w_value,
    check_column,
    key_cache,
    value_cache,
    page_table,
    lengths,
    tol_counts,
):
    seqs, width = tokens.shape
    head = key_cache.shape[-1]
    q_width, kv_width = w_query.shape[1], w_key.shape[1]
    total = q_width + 2 * kv_width
    q_heads = q_width // head
    depth = width // dp
    chips = dp // 2
    chunks = 5 if total % (5 * head) == 0 else 1
    chunk = total // chunks
    half_width = head // 2
    steps_index = jnp.arange(half_width, dtype=F32)
    inverse = ROPE_BASE ** (-2.0 * steps_index / head)
    angles = lengths.astype(F32)[:, None] * inverse[None, :]
    cosine, sine = jnp.cos(angles), jnp.sin(angles)
    cos_wide = jnp.concatenate([cosine, cosine], axis=1)
    sin_wide = jnp.concatenate([-sine, sine], axis=1)
    flat_keys = key_cache.reshape(key_cache.shape[0], -1, head)
    flat_values = value_cache.reshape(value_cache.shape[0], -1, head)

    smem = pl.BlockSpec(memory_space=pltpu.SMEM)
    vmem = pl.BlockSpec(memory_space=pltpu.VMEM)
    hbm = pl.BlockSpec(memory_space=pl.ANY)
    dma = pltpu.SemaphoreType.DMA
    attention, excess = pl.pallas_call(
        functools.partial(step_kernel, dp, tp),
        out_shape=(
            jax.ShapeDtypeStruct((seqs, q_width), BF16),
            jax.ShapeDtypeStruct((8, 128), F32),
        ),
        in_specs=[smem] * 3 + [vmem] * 5 + [hbm] * 5,
        out_specs=(vmem, vmem),
        scratch_shapes=[
            pltpu.VMEM((depth, total), BF16),
            pltpu.VMEM(flat_keys.shape, BF16),
            pltpu.VMEM(flat_values.shape, BF16),
            pltpu.VMEM((dp, seqs, depth), BF16),
            pltpu.VMEM((2, chips, seqs, depth), BF16),
            pltpu.VMEM((chunks, 2, chips * seqs, chunk), F32),
            pltpu.VMEM((chunks, chips * seqs, chunk), F32),
            pltpu.VMEM((chunks, chips - 1, seqs, chunk), F32),
            pltpu.VMEM((seqs, q_heads, head), F32),
            pltpu.VMEM((seqs, q_heads, head), F32),
            pltpu.VMEM((seqs, q_heads, head), F32),
            pltpu.VMEM((seqs, q_heads, head), F32),
            pltpu.VMEM((tp, seqs, 128), F32),
            pltpu.VMEM((seqs, 128), F32),
            pltpu.VMEM((dp, 8, 128), F32),
            pltpu.VMEM((8, 128), F32),
            dma((5,)),
            dma((2, chips)),
            dma((2, chips)),
            dma((chunks,)),
            dma((chunks,)),
            dma((chunks, chips - 1)),
            dma((chunks, chips - 1)),
            dma((tp,)),
            dma((tp,)),
            dma((dp,)),
            dma((dp,)),
        ],
        compiler_params=pltpu.CompilerParams(
            collective_id=0, has_side_effects=True, vmem_limit_bytes=60 * 1024 * 1024
        ),
    )(
        page_table,
        lengths,
        tol_counts,
        tokens,
        norm_gain.reshape(1, width),
        check_column.reshape(1, width),
        cos_wide,
        sin_wide,
        w_query,
        w_key,
        w_value,
        flat_keys,
        flat_values,
    )
    return attention, excess[0, 0]


def solution(mesh):
    return jax.shard_map(
        functools.partial(body, mesh.shape["dp"], mesh.shape["tensor"]),
        mesh=mesh,
        in_specs=(
            P("dp", None),
            P(),
            P("dp", "tensor"),
            P("dp", "tensor"),
            P("dp", "tensor"),
            P(),
            P("dp", None, "tensor", None),
            P("dp", None, "tensor", None),
            P("dp", None),
            P("dp"),
            P(),
        ),
        out_specs=(P("dp", "tensor"), P()),
        check_vma=False,
    )
```

time: 113 us -> 37.8 us (0.33)
  local copies, waits for them, and re-layouts: 44.3 us -> 5.36 us
  blocking collectives: 36.3 us -> 0 us
  Pallas kernels: 0 us -> 30 us
  between operations: 16.1 us -> 0.65 us
  matrix products: 10.8 us -> 0 us
  other arithmetic: 5.21 us -> 1.47 us
    gather x2 -> x0, local copies, waits for them, and re-layouts: 41.7 us -> none  [the longest x1 20.9 us: body(): value_cache[page_table].reshape(seq_rows, context, kv_here, head_size)]
    pallas_call x0 -> x1, Pallas kernels: none -> 30 us  [body(): pl.pallas_call(functools.partial(step_kernel, dp, tp), out_shape=(jax.Sha...]
    psum x2 -> x0, blocking collectives: 24.4 us -> none  [the longest x1 12.4 us: body(): excess = lax.psum(jnp.sum(token_excess), 'dp') / math.sqrt(all_rows)]
    all_to_all x1 -> x0, blocking collectives: 11.9 us -> none  [body(): lax.all_to_all(normed, 'dp', split_axis=1, concat_axis=0, tiled=True)]
    dot_general x7 -> x0, matrix products: 10.8 us -> none  [the longest x1 3.52 us: attend(): jnp.einsum('skgd,sckd->skgc', query_heads, cached_keys, preferred_element...]
    reshape x1 -> x2, local copies, waits for them, and re-layouts: 0.02 us -> 2.7 us  [the longest x1 1.35 us: body(): norm_gain.reshape(1, width)]
    reduce_sum x3 -> x0, other arithmetic: 1.5 us -> none  [the longest x1 1.13 us: normalize(): mean_square = jnp.mean(widened * widened, axis=1, keepdims=True)]
    convert_element_type x6 -> x1, other arithmetic: 1.93 us -> 0.66 us  [body(): angles = lengths.astype(F32)[:, None] * inverse[None, :]]
  transfers between devices with their start and end apart: 1 -> 0, of which waited for: 0 -> 0; matrix products, arithmetic and copies ran while one was open for 37% -> 0% of each run, Pallas kernels for 0% -> 0%
where the time goes in v1:
time: 37.8 us; the launch traced here: 37.5 us
  Pallas kernels  30 us (79%)
  local copies, waits for them, and re-layouts  5.36 us (14%)
  other arithmetic  1.47 us (4%)
  between operations  0.65 us (2%)
    pallas_call x1, Pallas kernels, body(): pl.pallas_call(functools.partial(step_kernel, dp, tp), out_shape=(jax.Sha...  30 us
    unnamed x1, local copies, waits for them, and re-layouts  1.47 us
    reshape x1, local copies, waits for them, and re-layouts, body(): norm_gain.reshape(1, width)  1.35 us
    reshape x1, local copies, waits for them, and re-layouts, body(): check_column.reshape(1, width)  1.35 us
    slice x1, local copies, waits for them, and re-layouts, body(): return (attention, excess[0, 0])  1.19 us

profile of v1, /device:TPU:0, one launch (start us, length us, event | category | flops | bytes accessed | tf_op | source)
XLA Modules:
  0.0 37.5 jit_solution(1808569522863929668)
XLA Ops:
  0.6 0.7 %convert_element_type.3 = f32[16]{0:T(128)S(1)} convert(s32[16]{0:T(128)} %lengths_ref.1) | non-fusion elementwise | flops 16 | bytes 128 | tf_op jit(solution)/shard_map/convert_element_type | solution.py:343
  1.3 0.1 fusion
  1.4 0.7 %pad_maximum_fusion = (f32[16,128]{1,0:T(8,128)}, f32[16,128]{1,0:T(8,128)}) fusion(f32[16,64]{1,0:T(8,128)S(1)} %get-tuple-element.8, f32[16,64]{1,0:T(8,128)S(1)} %get-tuple-element.7, f32[16,64]{1,0:T(8,128)S(1)} %get-tuple-element.6), kind=kLoop, calls=%fused_computation.2 | loop fusion | flops 4096 | bytes 28672 | tf_op jit(solution)/shard_map/concatenate | solution.py:345
  2.1 1.3 %reshape.22.gain_ref = bf16[1,8192]{1,0:T(2,128)(2,1)} reshape(bf16[8192]{0:T(1024)(128)(2,1)} %param.12) | data formatting | bytes 32768 | tf_op jit(solution)/shard_map/reshape | solution.py:399
  3.5 1.3 %reshape.23.check_ref = bf16[1,8192]{1,0:T(2,128)(2,1)} reshape(bf16[8192]{0:T(1024)(128)(2,1)} %param.16) | data formatting | bytes 32768 | tf_op jit(solution)/shard_map/reshape | solution.py:400
  4.8 30.0 %shard_map.122 = (bf16[16,2048]{1,0:T(8,128)(2,1)}, f32[8,128]{1,0:T(8,128)}) custom-call(s32[16,32]{1,0:T(8,128)} %table_ref.1, s32[16]{0:T(128)} %lengths_ref.1, s32[128]{0:T(128)} %counts_ref.1, bf16[16,8192]{1,0:T(8,128)(2,1)} %tokens_ref.1, bf16[1,8192]{1,0:T(2,128)(2,1)} %reshape.22.gain_ref, bf16[1,8192]{1,0:T(2,128)(2,1)} %reshape.23.check_ref, ...), custom_call_target="tpu_custom_call" | custom-call | tf_op jit(solution)/shard_map/pallas_call | solution.py:354
  34.8 1.2 %slice.3 = f32[1,1]{1,0:T(1,128)} slice(f32[8,128]{1,0:T(8,128)} %get-tuple-element.5), slice={[0:1], [0:1]} | slice | bytes 8 | tf_op jit(solution)/shard_map/slice | solution.py:409
  36.0 1.5 %copy.14 = bf16[16,2048]{1,0:T(8,128)(2,1)} copy(bf16[16,2048]{1,0:T(8,128)(2,1)} %get-tuple-element.13) | data formatting | bytes 131072
  (1 shorter events, 0.0 us)

commit v2 on v1

--- a/solution.py
+++ b/solution.py
@@ -15,6 +15,7 @@
 F32 = jnp.float32
 BF16 = jnp.bfloat16
 UNROLL = 4
+LANES = 128
 
 
 def step_kernel(
@@ -26,8 +27,6 @@
     tokens_ref,
     gain_ref,
     check_ref,
-    cos_ref,
-    sin_ref,
     wq_hbm,
     wk_hbm,
     wv_hbm,
@@ -49,6 +48,7 @@
     mixed,
     sums_all,
     sums_own,
+    shares,
     excess_all,
     excess_own,
     load_sems,
@@ -100,16 +100,17 @@
     for load in loads:
         load.start()
 
-    square = jnp.zeros((seqs, 1), F32)
-    for j in range(dp):
-        cols = pl.ds(j * depth, depth)
-        part = tokens_ref[:, cols].astype(F32)
-        square = square + jnp.sum(part * part, axis=1, keepdims=True)
-    scale = lax.rsqrt(square / width + EPSILON)
-    for j in range(dp):
-        cols = pl.ds(j * depth, depth)
-        outgoing[j] = (
-            tokens_ref[:, cols].astype(F32) * scale * gain_ref[:, cols].astype(F32)
+    square = jnp.zeros((seqs, LANES), F32)
+    for j in range(width // LANES):
+        part = tokens_ref[:, j * LANES : (j + 1) * LANES].astype(F32)
+        square = square + part * part
+    scale = lax.rsqrt(jnp.sum(square, axis=1, keepdims=True) / width + EPSILON)
+    gains = gain_ref[...].astype(F32)
+    for j in range(width // LANES):
+        part = tokens_ref[:, j * LANES : (j + 1) * LANES].astype(F32)
+        at = j * LANES % depth
+        outgoing[j * LANES // depth, :, at : at + LANES] = (
+            part * scale * gains[j : j + 1]
         ).astype(BF16)
     spread[0, 0] = outgoing[me]
 
@@ -132,12 +133,22 @@
             copy.start()
             a2a.append(copy)
 
-    check_sum = jnp.zeros((seqs, 1), F32)
-    for j in range(dp):
-        cols = pl.ds(j * depth, depth)
-        check_sum = check_sum + jnp.sum(
-            outgoing[j].astype(F32) * check_ref[:, cols].astype(F32), axis=1, keepdims=True
-        )
+    checks = check_ref[...].astype(F32)
+    checked = jnp.zeros((seqs, LANES), F32)
+    for j in range(width // LANES):
+        at = j * LANES % depth
+        part = outgoing[j * LANES // depth, :, at : at + LANES].astype(F32)
+        checked = checked + part * checks[j : j + 1]
+
+    seq_row = lax.broadcasted_iota(jnp.int32, (seqs, LANES), 0)
+    positions = jnp.zeros((seqs, LANES), F32)
+    for s in range(seqs):
+        positions = jnp.where(seq_row == s, lengths_ref[s].astype(F32), positions)
+    lane = lax.broadcasted_iota(jnp.int32, (seqs, head), 1)
+    step = (lane % (head // 2)).astype(F32)
+    angles = positions * jnp.exp(step * (-2.0 * math.log(ROPE_BASE) / head))
+    cosine = jnp.cos(angles)
+    sine = jnp.where(lane < head // 2, -1.0, 1.0) * jnp.sin(angles)
 
     for load in loads[:3]:
         load.wait()
@@ -165,6 +176,7 @@
         copy.start()
         pair_copies.append(copy)
         parts[c, 0] = product[:half]
+        return sum(product[:, i : i + LANES] for i in range(0, chunk, LANES))
 
     def pass_on(c):
         pair_copies[c].wait_recv()
@@ -182,27 +194,64 @@
             copy.start()
             chip_copies.append(copy)
 
+    def exchange(own, everyone, place, targets, send_sems, recv_sems):
+        everyone[place] = own[...]
+        copies = []
+        for k, target in enumerate(targets):
+            copy = pltpu.make_async_remote_copy(
+                src_ref=own,
+                dst_ref=everyone.at[place],
+                send_sem=send_sems.at[k],
+                recv_sem=recv_sems.at[k],
+                device_id=target,
+                device_id_type=MESH,
+            )
+            copy.start()
+            copies.append(copy)
+        return copies
+
+    row_sum = jnp.zeros((dp * seqs, LANES), F32)
     for c in range(chunks):
-        project(c)
+        row_sum = row_sum + project(c)
         if c >= 1:
             pass_on(c - 1)
+    for q in range(2):
+        for dc in range(chips):
+            owner = ((chip + chips - dc) % chips) * 2 + (core + q) % 2
+            at = (q * chips + dc) * seqs
+            share = row_sum[at : at + seqs]
+            if q == 0 and dc == 0:
+                share = share - jnp.where(zed == 0, checked, 0.0)
+            shares[owner] = share
+    turned_sums = jnp.transpose(shares[...].reshape(dp * seqs, LANES))
+    excess_own[...] = jnp.sum(turned_sums, axis=0, keepdims=True)
+    exc_copies = exchange(
+        excess_own, excess_all, me, [((me + k) % dp, zed) for k in range(1, dp)], exc_send, exc_recv
+    )
     pass_on(chunks - 1)
+    for copy in exc_copies:
+        copy.wait_recv()
+    group_sum = excess_all[0]
+    for k in range(1, dp):
+        group_sum = group_sum + excess_all[k]
+    sums_own[...] = group_sum
+    sum_copies = exchange(
+        sums_own, sums_all, zed, [(me, (zed + k) % tp) for k in range(1, tp)], sum_send, sum_recv
+    )
 
     def rotate(vector):
         return (
-            (vector * cos_ref[...] + pltpu.roll(vector, head // 2, 1) * sin_ref[...])
+            (vector * cosine + pltpu.roll(vector, head // 2, 1) * sine)
             .astype(BF16)
             .astype(F32)
         )
 
-    local_sum = jnp.zeros((seqs, 1), F32)
     for c in range(chunks):
         for copy in chip_copies[c * (chips - 1) : (c + 1) * (chips - 1)]:
             copy.wait_recv()
         own = parts[c, 0, pl.ds(0, seqs)] + from_pair[c, pl.ds(0, seqs)]
         for dc in range(1, chips):
             own = own + from_chips[c, dc - 1]
-        local_sum = local_sum + jnp.sum(own, axis=1, keepdims=True)
         for i in range(chunk // head):
             block = own[:, i * head : (i + 1) * head]
             index = c * (chunk // head) + i
@@ -219,21 +268,6 @@
                 for g in range(group):
                     new_values[:, k * group + g, :] = rounded
 
-    sums_own[...] = jnp.broadcast_to(local_sum, sums_own.shape)
-    sums_all[zed] = sums_own[...]
-    sum_copies = []
-    for k in range(1, tp):
-        copy = pltpu.make_async_remote_copy(
-            src_ref=sums_own,
-            dst_ref=sums_all.at[zed],
-            send_sem=sum_send.at[k],
-            recv_sem=sum_recv.at[k],
-            device_id=(me, (zed + k) % tp),
-            device_id_type=MESH,
-        )
-        copy.start()
-        sum_copies.append(copy)
-
     span = pages * page_rows
     column = lax.broadcasted_iota(jnp.int32, (q_heads, span), 1)
     row = lax.broadcasted_iota(jnp.int32, (q_heads, span), 0)
@@ -268,46 +302,19 @@
         mixed[s] = result / denominator
         return carry
 
-    middle = seqs // 2
-    lax.fori_loop(0, middle, one_sequence, 0, unroll=UNROLL)
+    lax.fori_loop(0, seqs, one_sequence, 0, unroll=UNROLL)
+
+    for h in range(q_heads):
+        out_ref[:, h * head : (h + 1) * head] = mixed[:, h, :].astype(BF16)
 
     for copy in sum_copies:
         copy.wait_recv()
-    row_sums = sums_all[0]
+    grand = sums_all[0]
     for k in range(1, tp):
-        row_sums = row_sums + sums_all[k]
-    seq_row = lax.broadcasted_iota(jnp.int32, (seqs, sums_own.shape[1]), 0)
-    counts = jnp.zeros(seq_row.shape, F32)
-    for s in range(seqs):
-        counts = jnp.where(seq_row == s, counts_ref[me * seqs + s].astype(F32), counts)
-    residual = (row_sums - check_sum) / math.sqrt(total * tp)
-    over = jnp.maximum(jnp.abs(residual) - TOL_STEP * counts, 0.0)
-    excess_own[...] = jnp.broadcast_to(jnp.sum(over, axis=0, keepdims=True), excess_own.shape)
-    excess_all[me] = excess_own[...]
-    exc_copies = []
-    for k in range(1, dp):
-        copy = pltpu.make_async_remote_copy(
-            src_ref=excess_own,
-            dst_ref=excess_all.at[me],
-            send_sem=exc_send.at[k],
-            recv_sem=exc_recv.at[k],
-            device_id=((me + k) % dp, zed),
-            device_id_type=MESH,
-        )
-        copy.start()
-        exc_copies.append(copy)
-
-    lax.fori_loop(middle, seqs, one_sequence, 0, unroll=UNROLL)
-
-    for h in range(q_heads):
-        out_ref[:, h * head : (h + 1) * head] = mixed[:, h, :].astype(BF16)
-
-    for copy in exc_copies:
-        copy.wait_recv()
-    grand = excess_all[0]
-    for k in range(1, dp):
-        grand = grand + excess_all[k]
-    excess_ref[...] = grand / math.sqrt(seqs * dp)
+        grand = grand + sums_all[k]
+    residual = grand / math.sqrt(total * tp)
+    over = jnp.maximum(jnp.abs(residual) - TOL_STEP * counts_ref[...].astype(F32), 0.0)
+    excess_ref[...] = jnp.sum(over, axis=1, keepdims=True) / math.sqrt(seqs * dp)
 
     for copy in a2a + pair_copies + chip_copies + sum_copies + exc_copies:
         copy.wait_send()
@@ -337,27 +344,20 @@
     chips = dp // 2
     chunks = 5 if total % (5 * head) == 0 else 1
     chunk = total // chunks
-    half_width = head // 2
-    steps_index = jnp.arange(half_width, dtype=F32)
-    inverse = ROPE_BASE ** (-2.0 * steps_index / head)
-    angles = lengths.astype(F32)[:, None] * inverse[None, :]
-    cosine, sine = jnp.cos(angles), jnp.sin(angles)
-    cos_wide = jnp.concatenate([cosine, cosine], axis=1)
-    sin_wide = jnp.concatenate([-sine, sine], axis=1)
     flat_keys = key_cache.reshape(key_cache.shape[0], -1, head)
     flat_values = value_cache.reshape(value_cache.shape[0], -1, head)
 
     smem = pl.BlockSpec(memory_space=pltpu.SMEM)
     vmem = pl.BlockSpec(memory_space=pltpu.VMEM)
-    hbm = pl.BlockSpec(memory_space=pl.ANY)
+    hbm = pl.BlockSpec(memory_space=pltpu.HBM)
     dma = pltpu.SemaphoreType.DMA
     attention, excess = pl.pallas_call(
         functools.partial(step_kernel, dp, tp),
         out_shape=(
             jax.ShapeDtypeStruct((seqs, q_width), BF16),
-            jax.ShapeDtypeStruct((8, 128), F32),
+            jax.ShapeDtypeStruct((1, 1), F32),
         ),
-        in_specs=[smem] * 3 + [vmem] * 5 + [hbm] * 5,
+        in_specs=[smem] * 2 + [vmem] * 4 + [hbm] * 5,
         out_specs=(vmem, vmem),
         scratch_shapes=[
             pltpu.VMEM((depth, total), BF16),
@@ -372,10 +372,11 @@
             pltpu.VMEM((seqs, q_heads, head), F32),
             pltpu.VMEM((seqs, q_heads, head), F32),
             pltpu.VMEM((seqs, q_heads, head), F32),
-            pltpu.VMEM((tp, seqs, 128), F32),
-            pltpu.VMEM((seqs, 128), F32),
-            pltpu.VMEM((dp, 8, 128), F32),
-            pltpu.VMEM((8, 128), F32),
+            pltpu.VMEM((tp, 1, dp * seqs), F32),
+            pltpu.VMEM((1, dp * seqs), F32),
+            pltpu.VMEM((dp, seqs, LANES), F32),
+            pltpu.VMEM((dp, 1, dp * seqs), F32),
+            pltpu.VMEM((1, dp * seqs), F32),
             dma((5,)),
             dma((2, chips)),
             dma((2, chips)),
@@ -394,12 +395,10 @@
     )(
         page_table,
         lengths,
-        tol_counts,
+        tol_counts.reshape(1, -1),
         tokens,
-        norm_gain.reshape(1, width),
-        check_column.reshape(1, width),
-        cos_wide,
-        sin_wide,
+        norm_gain.reshape(-1, LANES),
+        check_column.reshape(-1, LANES),
         w_query,
         w_key,
         w_value,

time: 37.8 us -> 32.7 us (0.87)
  local copies, waits for them, and re-layouts: 5.36 us -> 1.47 us
  between operations: 0.65 us -> 2.39 us
  other arithmetic: 1.47 us -> 0 us
  Pallas kernels: 30 us -> 28.6 us
    reshape x2 -> x0, local copies, waits for them, and re-layouts: 2.7 us -> none  [the longest x1 1.35 us: body(): norm_gain.reshape(1, width)]
    pallas_call x1, Pallas kernels: 30 us -> 28.6 us  [body(): pl.pallas_call(functools.partial(step_kernel, dp, tp), out_shape=(jax.Sha...]
    slice x1 -> x0, local copies, waits for them, and re-layouts: 1.19 us -> none  [body(): return (attention, excess[0, 0])]
    concatenate x1 -> x0, other arithmetic: 0.68 us -> none  [body(): cos_wide = jnp.concatenate([cosine, cosine], axis=1)]
    convert_element_type x1 -> x0, other arithmetic: 0.66 us -> none  [body(): angles = lengths.astype(F32)[:, None] * inverse[None, :]]
where the time goes in v2:
time: 32.7 us; the launch traced here: 32.5 us
  Pallas kernels  28.6 us (87%)
  between operations  2.39 us (7%)
  local copies, waits for them, and re-layouts  1.47 us (4%)
    pallas_call x1, Pallas kernels, body(): pl.pallas_call(functools.partial(step_kernel, dp, tp), out_shape=(jax.Sha...  28.6 us
    unnamed x1, local copies, waits for them, and re-layouts  1.47 us

profile of v2, /device:TPU:0, one launch (start us, length us, event | category | flops | bytes accessed | tf_op | source)
XLA Modules:
  0.0 32.5 jit_solution(17507563269420474158)
XLA Ops:
  0.6 28.6 %shard_map.122 = (bf16[16,2048]{1,0:T(8,128)(2,1)}, f32[1,1]{1,0:T(1,128)}) custom-call(s32[16,32]{1,0:T(8,128)} %table_ref.1, s32[16]{0:T(128)} %lengths_ref.1, s32[1,128]{1,0:T(1,128)} %bitcast.10, bf16[16,8192]{1,0:T(8,128)(2,1)} %tokens_ref.1, bf16[64,128]{1,0:T(8,128)(2,1)} %bitcast.8, bf16[64,128]{1,0:T(8,128)(2,1)} %bitcast.9, ...), custom_call_target="tpu_custom_call" | custom-call | tf_op jit(solution)/shard_map/pallas_call | solution.py:354
  29.2 1.5 %copy.15 = bf16[16,2048]{1,0:T(8,128)(2,1)} copy(bf16[16,2048]{1,0:T(8,128)(2,1)} %get-tuple-element.8) | data formatting | bytes 131072
